TPU v7x, 64 devices: a 2x2x8 block of a 4x4x8 slice. The times are simulated.
64 devices in a mesh: dp: 4 (over x, y), ep: 16 (over z, core).
Axes of the slice: x: 2, y: 2, z: 8, core: 2. Of those that a mesh axis runs over, the one named last changes fastest.
The devices are a block of a 4x4x8 slice.
Arguments:
- hidden: bfloat16 [16384, 2048], P(('dp', 'ep')), parts along dimension 0
- router_w: float32 [2048, 16], replicated
- expert_ids: int32 [16384, 2], P(('dp', 'ep')), parts along dimension 0
- w_gate: bfloat16 [16, 2048, 3200], P('ep')
- w_up: bfloat16 [16, 2048, 3200], P('ep')
- w_down: bfloat16 [16, 3200, 2048], P('ep')
- post_scale: float32 [2], replicated
Outputs:
- output: bfloat16 [16384, 2048], P(('dp', 'ep')), parts along dimension 0
There are 4 independent parts. A program takes and returns all parts, laid end to end along the dimension named above; an argument that names none is the same for every part.
All inputs are finite; a program needn't handle non-finite values.
Results may differ from a plain program's by a relative error of at most 0.001.
Values are sent between devices in bfloat16 or wider.
A program may use at most 768 MiB of HBM per device.

v0:
```python
import jax
import jax.numpy as jnp
from jax import lax
from jax.sharding import PartitionSpec as P


def route_tables(hidden, router_w, expert_ids, experts, capacity):
    tokens, choice_count = expert_ids.shape
    logits = jnp.dot(hidden.astype(jnp.float32), router_w, precision=lax.Precision.HIGHEST, preferred_element_type=jnp.float32)
    router_prob = jax.nn.softmax(logits, axis=-1)
    pick_mask = expert_ids[:, :, None] == jnp.arange(experts, dtype=jnp.int32)[None, None, :]
    picked = jnp.sum(jnp.where(pick_mask, router_prob[:, None, :], 0.0), axis=-1)
    gates = picked / jnp.sum(picked, axis=1, keepdims=True)
    pair_hot = pick_mask.reshape(tokens * choice_count, experts).astype(jnp.int32)
    earlier = jnp.cumsum(pair_hot, axis=0) - pair_hot
    slot_of = jnp.sum(earlier * pair_hot, axis=1).reshape(tokens, choice_count)
    slot_mask = slot_of[:, :, None] == jnp.arange(capacity, dtype=jnp.int32)[None, None, :]
    place = pick_mask[:, :, :, None] & slot_mask[:, :, None, :]
    return gates, place


def solution(mesh):
    ep_size = mesh.shape['ep']

    def local_step(hidden, router_w, expert_ids, w_gate, w_up, w_down, post_scale):
        tokens, model_width = hidden.shape
        local_experts = w_gate.shape[0]
        experts = local_experts * ep_size
        capacity = tokens // max(1, experts // 8)
        gates, place = route_tables(hidden, router_w, expert_ids, experts, capacity)
        token_table = jnp.any(place, axis=1).astype(jnp.bfloat16)
        outgoing = jnp.einsum('tec,td->ecd', token_table, hidden, preferred_element_type=jnp.float32).astype(jnp.bfloat16)
        incoming = lax.all_to_all(outgoing, 'ep', 0, 0, tiled=True).reshape(ep_size, local_experts, capacity, model_width)
        gate_in = jnp.einsum('slcd,ldf->slcf', incoming, w_gate, preferred_element_type=jnp.float32)
        up_in = jnp.einsum('slcd,ldf->slcf', incoming, w_up, preferred_element_type=jnp.float32)
        middle = (jax.nn.silu(gate_in) * up_in).astype(jnp.bfloat16)
        expert_out = jnp.einsum('slcf,lfd->slcd', middle, w_down, preferred_element_type=jnp.float32).astype(jnp.bfloat16)
        returned = lax.all_to_all(expert_out.reshape(experts, capacity, model_width), 'ep', 0, 0, tiled=True)
        pair_out = jnp.einsum('tkec,ecd->tkd', place.astype(jnp.bfloat16), returned, preferred_element_type=jnp.float32)
        mixed = jnp.sum(gates[:, :, None] * pair_out, axis=1)
        result = post_scale[0] * hidden.astype(jnp.float32) + post_scale[1] * mixed
        return result.astype(jnp.bfloat16)

    tok_spec = P(('dp', 'ep'))
    return jax.shard_map(local_step, mesh=mesh, in_specs=(tok_spec, P(), tok_spec, P('ep'), P('ep'), P('ep'), P()), out_specs=tok_spec, check_vma=False)
```

profile of v0, /device:TPU:28, one launch (start us, length us, event | category | flops | bytes accessed | tf_op | source)
XLA Modules:
  0.0 520.1 jit_solution(13248488681532579804)
XLA Ops:
  0.0 0.0 copy-start
  0.0 0.8 copy.12
  0.9 0.1 eq.58
  1.0 0.1 eq.62
  1.1 0.7 iota_compare_fusion.3
  1.9 1.2 reduce-window.6
  3.0 0.2 slice_reduce_fusion
  3.3 0.1 fusion.28
  3.4 0.1 eq.66
  3.5 0.1 copy.15
  3.6 0.1 iota_compare_fusion
  3.8 0.0 copy-start.2
  3.8 0.6 copy-done.2
  4.4 1.7 and_reduce_fusion
  6.1 0.0 copy-done.4
  6.1 3.6 convolution_convert_fusion
  9.7 194.5 %all_to_all.10 = bf16[16,128,2048]{2,1,0:T(8,128)(2,1)S(1)} all-to-all(bf16[16,128,2048]{2,1,0:T(8,128)(2,1)S(1)} %convolution_convert_fusion), channel_id=1, replica_groups=mesh['dp'=4,'ep'=16] {'ep'}, dimensions={0} | all-to-all | bytes 16777216 | tf_op jit(solution)/shard_map/all_to_all | solution.py:33
  204.2 36.3 %fusion.7 = f32[16,128,3200]{2,1,0:T(8,128)} fusion(bf16[16,128,2048]{2,1,0:T(8,128)(2,1)S(1)} %all_to_all.10, bf16[1,2048,3200]{2,1,0:T(8,128)(2,1)} %param.11), kind=kOutput, calls=%fused_computation.10 | convolution fusion | flops 26843545600 | bytes 47710208 | tf_op jit(solution)/shard_map/slcd,ldf->slcf/dot_general | solution.py:35
  240.5 38.4 %fusion = bf16[16,1,128,3200]{3,2,0,1:T(8,128)(2,1)} fusion(f32[16,128,3200]{2,1,0:T(8,128)} %fusion.7, bf16[16,128,2048]{2,1,0:T(8,128)(2,1)S(1)} %all_to_all.10, bf16[1,2048,3200]{2,1,0:T(8,128)(2,1)} %param.10), kind=kOutput, calls=%fused_computation.1 | convolution fusion | flops 26882867200 | bytes 60817408 | tf_op jit(solution)/shard_map/slcd,ldf->slcf/dot_general | solution.py:34
  278.8 36.3 %fusion.12 = bf16[16,128,2048]{2,1,0:T(8,128)(2,1)} fusion(bf16[1,3200,2048]{2,1,0:T(8,128)(2,1)} %param.12, bf16[16,1,128,3200]{3,2,0,1:T(8,128)(2,1)} %fusion), kind=kOutput, calls=%fused_computation.15 | convolution fusion | flops 26847739904 | bytes 34603008 | tf_op jit(solution)/shard_map/slcf,lfd->slcd/dot_general | solution.py:37
  315.1 0.0 copy-start.3
  315.1 0.0 copy-start.5
  315.1 5.3 %all-to-all-start.1 = ((bf16[16,128,2048]{2,1,0:T(8,128)(2,1)}), bf16[16,128,2048]{2,1,0:T(8,128)(2,1)}, u32[]{:S(2)}, u32[]{:S(2)}) async-start(bf16[16,128,2048]{2,1,0:T(8,128)(2,1)} %fusion.12), calls=%async_computation.1 | async-start | bytes 16777216 | tf_op jit(solution)/shard_map/all_to_all | solution.py:38
  320.4 0.0 copy-done.7
  320.4 0.7 fusion.32
  321.1 0.0 copy-done
  321.1 0.9 fusion.33
  322.1 0.0 copy-done.6
  322.1 187.2 %all-to-all-done.1 = bf16[16,128,2048]{2,1,0:T(8,128)(2,1)} async-done(((bf16[16,128,2048]{2,1,0:T(8,128)(2,1)}), bf16[16,128,2048]{2,1,0:T(8,128)(2,1)}, u32[]{:S(2)}, u32[]{:S(2)}) %all-to-all-start.1) | async-done | bytes 8388640 | tf_op jit(solution)/shard_map/all_to_all | solution.py:38
  509.3 0.0 copy-done.5
  509.3 8.2 %fusion.18 = f32[256,2048]{1,0:T(8,128)S(1)} fusion(bf16[16,128,2048]{2,1,0:T(8,128)(2,1)} %all-to-all-done.1, f32[256,2]{0,1:T(2,128)S(1)} %broadcast_divide_fusion, pred[256,2,128]{2,0,1:T(8,128)(4,1)S(1)} %copy-done.3, pred[256,2,16]{0,2,1:T(8,128)(4,1)S(1)} %copy-done.5), kind=kOutput, calls=%fused_computation.20 | convolution fusion | flops 4297588736 | bytes 10561536 | tf_op jit(solution)/shard_map/tkec,ecd->tkd/dot_general | solution.py:39
  517.5 2.6 add_convert_fusion
  (13 shorter events, 0.1 us)
Async XLA Ops:
  0.0 321.1 %copy-start = (f32[2048,16]{0,1:T(8,128)S(1)}, f32[2048,16]{0,1:T(8,128)}, u32[]{:S(2)}) copy-start(f32[2048,16]{0,1:T(8,128)} %param.8) | copy-start | bytes 393220
  1.8 4.2 copy-start.4
  3.8 0.6 copy-start.2
  315.1 5.3 %copy-start.7 = (f32[2]{0:T(128)S(1)}, f32[2]{0:T(128)}, u32[]{:S(2)}) copy-start(f32[2]{0:T(128)} %param.13) | copy-start | bytes 28
  315.1 6.0 %copy-start.1 = (bf16[256,2048]{1,0:T(8,128)(2,1)S(1)}, bf16[256,2048]{1,0:T(8,128)(2,1)}, u32[]{:S(2)}) copy-start(bf16[256,2048]{1,0:T(8,128)(2,1)} %param.7) | copy-start | bytes 3145732
  315.1 7.0 %copy-start.6 = (s32[256,2]{0,1:T(2,128)S(1)}, s32[256,2]{0,1:T(2,128)}, u32[]{:S(2)}) copy-start(s32[256,2]{0,1:T(2,128)} %param.9) | copy-start | bytes 6148
  315.1 194.2 %copy-start.3 = (pred[256,2,128]{2,0,1:T(8,128)(4,1)S(1)}, pred[256,2,128]{2,0,1:T(8,128)(4,1)}, u32[]{:S(2)}) copy-start(pred[256,2,128]{2,0,1:T(8,128)(4,1)} %copy-done.2) | copy-start | bytes 196612
  315.1 194.2 %copy-start.5 = (pred[256,2,16]{0,2,1:T(8,128)(4,1)S(1)}, pred[256,2,16]{0,2,1:T(8,128)(4,1)}, u32[]{:S(2)}) copy-start(pred[256,2,16]{0,2,1:T(8,128)(4,1)} %copy-done.4) | copy-start | bytes 24580
  315.1 194.2 %all-to-all-start.1 = ((bf16[16,128,2048]{2,1,0:T(8,128)(2,1)}), bf16[16,128,2048]{2,1,0:T(8,128)(2,1)}, u32[]{:S(2)}, u32[]{:S(2)}) async-start(bf16[16,128,2048]{2,1,0:T(8,128)(2,1)} %fusion.12), calls=%async_computation.1 | async-start | bytes 16777216 | tf_op jit(solution)/shard_map/all_to_all | solution.py:38
where the time goes:
time: 522 us; the launch traced here: 520 us
  blocking collectives  194 us (37%)
  waiting for transfers between devices  187 us (36%)
  matrix products  124 us (24%)
  other arithmetic  6.48 us (1%)
  starting transfers between devices  5.27 us (1%)
    all_to_all x1, blocking collectives, local_step(): lax.all_to_all(outgoing, 'ep', 0, 0, tiled=True)  194 us
    all_to_all x1, waiting for transfers between devices, local_step(): lax.all_to_all(expert_out.reshape(experts, capacity, model_width), 'ep',...  187 us
    dot_general x1, matrix products, local_step(): jnp.einsum('slcd,ldf->slcf', incoming, w_gate, preferred_element_type=jnp...  38.4 us
    dot_general x1, matrix products, local_step(): jnp.einsum('slcd,ldf->slcf', incoming, w_up, preferred_element_type=jnp.f...  36.3 us
    dot_general x1, matrix products, local_step(): jnp.einsum('slcf,lfd->slcd', middle, w_down, preferred_element_type=jnp.f...  36.3 us
  transfers between devices with their start and end apart: 1, of which 1 were waited for; matrix products, arithmetic and copies ran while one was open for 0% of the time, Pallas kernels for 0%

commit v1 on v0

v1 whole, which is shorter than its diff:
```python
import functools

import jax
import jax.numpy as jnp
from jax import lax
from jax.experimental import pallas as pl
from jax.experimental.pallas import tpu as pltpu
from jax.sharding import PartitionSpec as P

MESH = pl.DeviceIdType.MESH
SUBS = 4
DIRECT = 24
PITCH = 32
F32, BF16 = jnp.float32, jnp.bfloat16


def tiles(width, size):
    return [(off, min(size, width - off)) for off in range(0, width, size)]


def moe_kernel(ep, cap, hid, rwt, idt, w1, w3, w2, ps, out, flag, agr, ags,
               w1v, w3v, w2v, xr, xs, xsel, mid, ycat, ysib, rs, sec, tmat, cr, cs, gat,
               w1s, w3s, w2s, ldr, lds, agsend, agrecv, sibsend, sibrecv,
               cse, crv, sse, srv, yss, ysr, s1s, s2s, secr, rss, rsr, outs):
    tokens, width = hid.shape
    ffn = w1.shape[2]
    chips = ep // 2
    sub = tokens // SUBS
    me = lax.axis_index('ep')
    chip, core = me // 2, lax.rem(me, 2)
    way = 1 - 2 * core
    sib = me + way
    d_tiles, f_tiles = tiles(width, 512), tiles(ffn, 512)

    def on_chip(steps):
        return lax.rem(chip + steps * way + chips, chips)

    nxt = on_chip(1) * 2 + core

    def rows(q):
        return pl.ds(q * sub, sub)

    def dev(i):
        return dict(device_id={'ep': i}, device_id_type=MESH)

    def ring_sub(k, q, first=False):
        src = hid.at[rows(q)] if first else agr.at[k, rows(q)]
        return pltpu.make_async_remote_copy(src, agr.at[k + 1, rows(q)], agsend.at[k, q], agrecv.at[k + 1, q], **dev(nxt))

    def sib_sub(k, q, first=False):
        src = hid.at[rows(q)] if first else agr.at[k, rows(q)]
        return pltpu.make_async_remote_copy(src, ags.at[k, rows(q)], sibsend.at[k, q], sibrecv.at[k, q], **dev(sib))

    def code_ring(k):
        return pltpu.make_async_remote_copy(cr.at[k], cr.at[k + 1], cse.at[k], crv.at[k + 1], **dev(nxt))

    def code_sib(k):
        return pltpu.make_async_remote_copy(cr.at[k], cs.at[k], sse.at[k], srv.at[k], **dev(sib))

    def load_r(k, q, first=False):
        src = hid.at[rows(q)] if first else agr.at[k, rows(q)]
        return pltpu.make_async_copy(src, xr.at[rows(q)], ldr.at[q])

    def load_s(k, q):
        return pltpu.make_async_copy(ags.at[k, rows(q)], xs.at[rows(q)], lds.at[q])

    def y_copy(k):
        return pltpu.make_async_remote_copy(ysib.at[lax.rem(k, 2)], ycat.at[k, pl.ds(cap, cap)], yss.at[k], ysr.at[k], **dev(sib))

    def slot(e):
        return sec.at[pl.ds(pl.multiple_of(e * PITCH, PITCH), DIRECT)]

    def direct_r(k):
        return pltpu.make_async_remote_copy(ycat.at[k, pl.ds(0, DIRECT)], slot(me), s1s.at[k], secr.at[me], **dev(on_chip(-k) * 2 + core))

    def direct_s(k):
        return pltpu.make_async_remote_copy(ysib.at[lax.rem(k, 2), pl.ds(0, DIRECT)], slot(me), s2s.at[k], secr.at[me], **dev(on_chip(k) * 2 + 1 - core))

    def rs_copy(k, q, first=False):
        src = xsel.at[rows(q)] if first else rs.at[k - 2, rows(q)]
        return pltpu.make_async_remote_copy(src, rs.at[k - 1, rows(q)], rss.at[k, q], rsr.at[k + 1, q], **dev(nxt))

    def rs_arrival(k, q):
        return pltpu.make_async_remote_copy(xsel.at[rows(q)], rs.at[k - 2, rows(q)], rss.at[k - 1, q], rsr.at[k, q], **dev(nxt))

    def load_up(i):
        off, size = f_tiles[i]
        cols = pl.ds(off, size)
        return (pltpu.make_async_copy(w1.at[0, :, cols], w1v.at[:, cols], w1s.at[i]),
                pltpu.make_async_copy(w3.at[0, :, cols], w3v.at[:, cols], w3s.at[i]))

    def load_down(i):
        off, size = d_tiles[i]
        cols = pl.ds(off, size)
        return pltpu.make_async_copy(w2.at[0, :, cols], w2v.at[:, cols], w2s.at[i])

    for q in range(SUBS):
        load_r(0, q, True).start()
    for i in range(len(f_tiles)):
        for copy in load_up(i):
            copy.start()
    for i in range(len(d_tiles)):
        load_down(i).start()
    sec[...] = jnp.zeros_like(sec)

    barrier = pltpu.get_barrier_semaphore()
    for d in range(1, ep):
        pl.semaphore_signal(barrier, inc=1, **dev(lax.rem(me + d, ep)))
    pl.semaphore_wait(barrier, ep - 1)

    for q in range(SUBS):
        ring_sub(0, q, True).start()
    for q in range(SUBS):
        sib_sub(0, q, True).start()

    row0, row1 = idt[0:1, :], idt[1:2, :]
    eio = lax.broadcasted_iota(jnp.int32, (ep, tokens), 0)
    m0 = jnp.where(eio == row0, 1.0, 0.0)
    m1 = jnp.where(eio == row1, 1.0, 0.0)
    cnt = jnp.sum(m0 + m1, axis=1, keepdims=True)
    lead = jnp.broadcast_to(jnp.sum((m0 - m1) * cnt, axis=0, keepdims=True), (ep, tokens))
    mp = jnp.where(lead >= 0, m0, m1)
    ms = m0 + m1 - mp
    earlier = jnp.where(lax.broadcasted_iota(jnp.int32, (tokens, tokens), 0) < lax.broadcasted_iota(jnp.int32, (tokens, tokens), 1), 1.0, 0.0).astype(BF16)
    rank_p = jnp.dot(mp.astype(BF16), earlier, preferred_element_type=F32)
    rank_s = jnp.dot(ms.astype(BF16), earlier, preferred_element_type=F32)
    n_s = jnp.sum(ms, axis=1, keepdims=True)
    ef = eio.astype(F32)
    code_p = jnp.sum(mp * (ef * cap + n_s + rank_p), axis=0, keepdims=True)
    code_s = jnp.sum(ms * (ef * cap + rank_s), axis=0, keepdims=True)
    place_s = jnp.sum(ms * (ef * PITCH + rank_s), axis=0, keepdims=True)
    r8 = lax.broadcasted_iota(jnp.int32, (8, tokens), 0)
    cr[0] = jnp.where(r8 == 0, code_p, jnp.where(r8 == 1, code_s, 0.0))

    for q in range(SUBS):
        load_r(0, q, True).wait()
    code_ring(0).start()
    code_sib(0).start()
    logits = jnp.zeros((ep, tokens), F32)
    for off, size in d_tiles:
        logits += lax.dot_general(rwt[:, off:off + size], xr[:, off:off + size].astype(F32), (((1,), (1,)), ((), ())),
                                  precision=lax.Precision.HIGHEST, preferred_element_type=F32)
    grown = jnp.exp(logits - jnp.max(logits, axis=0, keepdims=True))
    prob = grown / jnp.sum(grown, axis=0, keepdims=True)
    prob_p = jnp.sum(mp * prob, axis=0, keepdims=True)
    prob_s = jnp.sum(ms * prob, axis=0, keepdims=True)
    total = prob_p + prob_s
    r128 = lax.broadcasted_iota(jnp.int32, (128, tokens), 0)
    gat[...] = jnp.where(r128 == 0, prob_p / total, jnp.where(r128 == 1, prob_s / total, jnp.where(r128 == 2, place_s, 0.0))).T

    for q in range(SUBS):
        sib_sub(0, q, True).wait_recv()
        load_s(0, q).start()
    for q in range(SUBS):
        load_s(0, q).wait()
    code_sib(0).wait_recv()

    mine = (me * cap).astype(F32) + lax.broadcasted_iota(jnp.int32, (cap, tokens), 0).astype(F32)

    def pick(codes, block, base):
        hot = jnp.where((codes[0:1, :] == mine) | (codes[1:2, :] == mine), 1.0, 0.0).astype(BF16)
        for off, size in d_tiles:
            xsel[base:base + cap, off:off + size] = jnp.dot(hot, block[:, off:off + size], preferred_element_type=F32).astype(BF16)

    def poll(k, q):
        if q < SUBS:
            ring_sub(k - 1, q).wait_recv()

            @pl.when(k < chips - 1)
            def _():
                ring_sub(k, q).start()
            sib_sub(k, q).start()
            load_r(k, q).start()
        if q == 0:
            code_ring(k - 1).wait_recv()

            @pl.when(k < chips - 1)
            def _():
                code_ring(k).start()
            code_sib(k).start()
        if q > 0:
            sib_sub(k, q - 1).wait_recv()
            load_s(k, q - 1).start()
        if q == SUBS:
            code_sib(k).wait_recv()

    up_count = len(f_tiles)
    pieces = up_count + len(d_tiles)
    poll_at = {}
    for q in range(SUBS + 1):
        poll_at.setdefault(min(pieces - 1, (q + 1) * pieces // (SUBS + 1) - 1), []).append(q)

    def expert_step(k, carry):
        @pl.when(k > 0)
        def _():
            for q in range(SUBS):
                load_r(k, q).wait()
                load_s(k, q).wait()
        pick(cr[k], xr, 0)
        pick(cs[k], xs, cap)

        @pl.when(k >= 2)
        def _():
            y_copy(k - 2).wait_send()
            direct_s(k - 2).wait_send()
        for piece in range(pieces):
            if piece < up_count:
                off, size = f_tiles[piece]

                @pl.when(k == 0)
                def _():
                    for copy in load_up(piece):
                        copy.wait()
                gate = jnp.dot(xsel[...], w1v[:, off:off + size], preferred_element_type=F32)
                up = jnp.dot(xsel[...], w3v[:, off:off + size], preferred_element_type=F32)
                mid[:, off:off + size] = (jax.nn.silu(gate) * up).astype(BF16)
            else:
                off, size = d_tiles[piece - up_count]

                @pl.when(k == 0)
                def _():
                    load_down(piece - up_count).wait()
                y = jnp.dot(mid[...], w2v[:, off:off + size], preferred_element_type=F32).astype(BF16)
                ycat[k, 0:cap, off:off + size] = y[:cap]
                ysib[lax.rem(k, 2), :, off:off + size] = y[cap:]
            for q in poll_at.get(piece, []):
                @pl.when(k < chips - 1)
                def _():
                    poll(k + 1, q)
        y_copy(k).start()
        direct_s(k).start()

        @pl.when(k > 0)
        def _():
            direct_r(k).start()
        return carry

    lax.fori_loop(0, chips, expert_step, 0)

    for q in range(SUBS):
        load_r(0, q, True).start()
    s_io = lax.broadcasted_iota(jnp.int32, (2 * cap, tokens), 0)
    pair = jnp.where(s_io < cap, me * cap + s_io, sib * cap + s_io - cap).astype(F32)

    def place(k):
        tmat[...] = jnp.where(cr[k][0:1, :] == pair, 1.0, 0.0).T.astype(BF16)

    place(1)
    y_copy(1).wait_recv()
    for q in range(SUBS):
        for off, size in d_tiles:
            xsel[q * sub:(q + 1) * sub, off:off + size] = jnp.dot(
                tmat[q * sub:(q + 1) * sub, :], ycat[1, :, off:off + size], preferred_element_type=F32).astype(BF16)
        rs_copy(1, q, True).start()

    def ring_step(k, carry):
        place(k)
        y_copy(k).wait_recv()
        for q in range(SUBS):
            rs_arrival(k, q).wait_recv()
            for off, size in d_tiles:
                part = jnp.dot(tmat[q * sub:(q + 1) * sub, :], ycat[k, :, off:off + size], preferred_element_type=F32)
                old = rs[k - 2, q * sub:(q + 1) * sub, off:off + size]
                rs[k - 2, q * sub:(q + 1) * sub, off:off + size] = (part + old.astype(F32)).astype(BF16)
            rs_copy(k, q).start()
        return carry

    lax.fori_loop(2, chips, ring_step, 0)

    for k in (chips - 2, chips - 1):
        y_copy(k).wait_send()
        direct_s(k).wait_send()
    worst = jnp.zeros((1, tokens), F32)
    for k in range(chips):
        for codes in (cr, cs):
            code = codes[k][1:2, :]
            worst = jnp.maximum(worst, code - jnp.floor(code * (1.0 / cap)) * cap)
    flag[...] = jnp.broadcast_to(jnp.max(worst, axis=1, keepdims=True), flag.shape)

    place(0)
    y_copy(0).wait_recv()
    sec[pl.ds(pl.multiple_of(me * PITCH, PITCH), DIRECT), :] = ycat[0, 0:DIRECT, :]
    for e in range(ep):
        @pl.when(me != e)
        def _():
            pltpu.make_async_remote_copy(ycat.at[0, pl.ds(0, DIRECT)], slot(e), s1s.at[0], secr.at[e], **dev(sib)).wait_recv()
    lanes = lax.broadcasted_iota(jnp.int32, (tokens, ep * PITCH), 1).astype(F32)
    sel = jnp.where(lanes == gat[:, 2:3], 1.0, 0.0).astype(BF16)
    for off, size in d_tiles:
        got = jnp.dot(sel, sec[:, off:off + size], preferred_element_type=F32).astype(BF16)
        for half in range(2):
            ysib[half, :, off:off + size] = got[half * cap:(half + 1) * cap]
    for q in range(SUBS):
        load_r(0, q, True).wait()
    alpha, beta = ps[0], ps[1]
    per_half = cap // sub
    for q in range(SUBS):
        rs_arrival(chips, q).wait_recv()
        at = slice(q * sub, (q + 1) * sub)
        base = (q % per_half) * sub
        for off, size in d_tiles:
            cols = slice(off, off + size)
            main = jnp.dot(tmat[at, :], ycat[0, :, cols], preferred_element_type=F32) + rs[chips - 2, at, cols].astype(F32)
            other = ysib[q // per_half, base:base + sub, cols].astype(F32)
            mixed = gat[at, 0:1] * main + gat[at, 1:2] * other
            xs[at, cols] = (alpha * xr[at, cols].astype(F32) + beta * mixed).astype(BF16)
        pltpu.make_async_copy(xs.at[rows(q)], out.at[rows(q)], outs.at[q]).start()

    def drain(k, carry):
        for q in range(SUBS):
            @pl.when(k < chips - 1)
            def _():
                ring_sub(k, q).wait_send()
            sib_sub(k, q).wait_send()

            @pl.when(k > 0)
            def _():
                rs_arrival(k + 1, q).wait_send()

        @pl.when(k < chips - 1)
        def _():
            code_ring(k).wait_send()
        code_sib(k).wait_send()

        @pl.when(k > 0)
        def _():
            direct_r(k).wait_send()
        return carry

    lax.fori_loop(0, chips, drain, 0)
    for q in range(SUBS):
        pltpu.make_async_copy(xs.at[rows(q)], out.at[rows(q)], outs.at[q]).wait()


def route_tables(hidden, router_w, expert_ids, experts, capacity):
    tokens, choice_count = expert_ids.shape
    logits = jnp.dot(hidden.astype(F32), router_w, precision=lax.Precision.HIGHEST, preferred_element_type=F32)
    router_prob = jax.nn.softmax(logits, axis=-1)
    pick_mask = expert_ids[:, :, None] == jnp.arange(experts, dtype=jnp.int32)[None, None, :]
    picked = jnp.sum(jnp.where(pick_mask, router_prob[:, None, :], 0.0), axis=-1)
    gates = picked / jnp.sum(picked, axis=1, keepdims=True)
    pair_hot = pick_mask.reshape(tokens * choice_count, experts).astype(jnp.int32)
    earlier = jnp.cumsum(pair_hot, axis=0) - pair_hot
    slot_of = jnp.sum(earlier * pair_hot, axis=1).reshape(tokens, choice_count)
    slot_mask = slot_of[:, :, None] == jnp.arange(capacity, dtype=jnp.int32)[None, None, :]
    place = pick_mask[:, :, :, None] & slot_mask[:, :, None, :]
    return gates, place


def padded_step(ep, hidden, router_w, expert_ids, w_gate, w_up, w_down, post_scale):
    tokens, width = hidden.shape
    capacity = tokens // max(1, ep // 8)
    gates, place = route_tables(hidden, router_w, expert_ids, ep, capacity)
    token_table = jnp.any(place, axis=1).astype(BF16)
    outgoing = jnp.einsum('tec,td->ecd', token_table, hidden, preferred_element_type=F32).astype(BF16)
    incoming = lax.all_to_all(outgoing, 'ep', 0, 0, tiled=True).reshape(ep * capacity, width)
    gate_in = jnp.dot(incoming, w_gate[0], preferred_element_type=F32)
    up_in = jnp.dot(incoming, w_up[0], preferred_element_type=F32)
    middle = (jax.nn.silu(gate_in) * up_in).astype(BF16)
    expert_out = jnp.dot(middle, w_down[0], preferred_element_type=F32).astype(BF16)
    returned = lax.all_to_all(expert_out.reshape(ep, capacity, width), 'ep', 0, 0, tiled=True)
    pair_out = jnp.einsum('tkec,ecd->tkd', place.astype(BF16), returned, preferred_element_type=F32)
    mixed = jnp.sum(gates[:, :, None] * pair_out, axis=1)
    result = post_scale[0] * hidden.astype(F32) + post_scale[1] * mixed
    return result.astype(BF16)


def solution(mesh):
    ep = mesh.shape['ep']

    def local_step(hidden, router_w, expert_ids, w_gate, w_up, w_down, post_scale):
        tokens, width = hidden.shape
        ffn = w_gate.shape[2]
        chips = ep // 2
        cap = tokens // max(1, ep // 8)
        anyspace = pl.BlockSpec(memory_space=pl.ANY)
        vmem = pl.BlockSpec(memory_space=pltpu.VMEM)
        dma = pltpu.SemaphoreType.DMA
        n_f, n_d = len(tiles(ffn, 512)), len(tiles(width, 512))
        block = jax.ShapeDtypeStruct((chips, tokens, width), BF16)
        result, flag, _, _ = pl.pallas_call(
            functools.partial(moe_kernel, ep, cap),
            out_shape=(jax.ShapeDtypeStruct((tokens, width), BF16), jax.ShapeDtypeStruct((8, 128), F32), block, block),
            in_specs=[anyspace, vmem, vmem, anyspace, anyspace, anyspace, pl.BlockSpec(memory_space=pltpu.SMEM)],
            out_specs=(anyspace, vmem, anyspace, anyspace),
            scratch_shapes=[
                pltpu.VMEM((width, ffn), BF16), pltpu.VMEM((width, ffn), BF16), pltpu.VMEM((ffn, width), BF16),
                pltpu.VMEM((tokens, width), BF16), pltpu.VMEM((tokens, width), BF16), pltpu.VMEM((2 * cap, width), BF16),
                pltpu.VMEM((2 * cap, ffn), BF16),
                pltpu.VMEM((chips, 2 * cap, width), BF16), pltpu.VMEM((2, cap, width), BF16),
                pltpu.VMEM((chips - 1, tokens, width), BF16), pltpu.VMEM((ep * PITCH, width), BF16),
                pltpu.VMEM((tokens, 2 * cap), BF16),
                pltpu.VMEM((chips, 8, tokens), F32), pltpu.VMEM((chips, 8, tokens), F32), pltpu.VMEM((tokens, 128), F32),
                dma((n_f,)), dma((n_f,)), dma((n_d,)), dma((SUBS,)), dma((SUBS,)),
                dma((chips, SUBS)), dma((chips, SUBS)), dma((chips, SUBS)), dma((chips, SUBS)),
                dma((chips,)), dma((chips,)), dma((chips,)), dma((chips,)),
                dma((chips,)), dma((chips,)), dma((chips,)), dma((chips,)), dma((ep,)),
                dma((chips, SUBS)), dma((chips + 1, SUBS)), dma((SUBS,)),
            ],
            compiler_params=pltpu.CompilerParams(collective_id=0, has_side_effects=True, vmem_limit_bytes=67043328),
            name='moe_ring',
        )(hidden, router_w.T, expert_ids.T, w_gate, w_up, w_down, post_scale)
        return lax.cond(
            flag[0, 0] >= DIRECT,
            lambda: padded_step(ep, hidden, router_w, expert_ids, w_gate, w_up, w_down, post_scale),
            lambda: result)

    tok_spec = P(('dp', 'ep'))
    return jax.shard_map(local_step, mesh=mesh, in_specs=(tok_spec, P(), tok_spec, P('ep'), P('ep'), P('ep'), P()), out_specs=tok_spec, check_vma=False)
```

time: 522 us -> 231 us (0.44)
  Pallas kernels: 0 us -> 226 us
  blocking collectives: 194 us -> 0 us
  waiting for transfers between devices: 187 us -> 0 us
  matrix products: 124 us -> 0 us
  other arithmetic: 6.48 us -> 0 us
  starting transfers between devices: 5.27 us -> 0 us
    pallas_call x0 -> x1, Pallas kernels: none -> 226 us  [local_step(): pl.pallas_call(functools.partial(moe_kernel, ep, cap), out_shape=(jax.Sha...]
    all_to_all x1 -> x0, blocking collectives: 194 us -> none  [local_step(): lax.all_to_all(outgoing, 'ep', 0, 0, tiled=True)]
    all_to_all x1 -> x0, waiting for transfers between devices: 187 us -> none  [local_step(): lax.all_to_all(expert_out.reshape(experts, capacity, model_width), 'ep',...]
    dot_general x6 -> x0, matrix products: 124 us -> none  [the longest x1 38.4 us: local_step(): jnp.einsum('slcd,ldf->slcf', incoming, w_gate, preferred_element_type=jnp...]
    all_to_all x1 -> x0, starting transfers between devices: 5.27 us -> none  [local_step(): lax.all_to_all(expert_out.reshape(experts, capacity, model_width), 'ep',...]
  transfers between devices with their start and end apart: 1 -> 0, of which waited for: 1 -> 0; matrix products, arithmetic and copies ran while one was open for 0% -> 0% of each run, Pallas kernels for 0% -> 0%
where the time goes in v1:
time: 231 us
  Pallas kernels  226 us (98%)
  local copies, waits for them, and re-layouts  3.49 us (2%)
    pallas_call x1, Pallas kernels, local_step(): pl.pallas_call(functools.partial(moe_kernel, ep, cap), out_shape=(jax.Sha...  226 us

profile of v1, /device:TPU:28, one launch (start us, length us, event | category | flops | bytes accessed | tf_op | source)
XLA Modules:
  0.0 230.9 jit_solution(9575870448665592676)
XLA Ops:
  0.0 226.4 %moe_ring.1 = (bf16[256,2048]{1,0:T(8,128)(2,1)}, f32[8,128]{1,0:T(8,128)}, bf16[8,256,2048]{2,1,0:T(8,128)(2,1)}, bf16[8,256,2048]{2,1,0:T(8,128)(2,1)}) custom-call(bf16[256,2048]{1,0:T(8,128)(2,1)} %hid.1, f32[16,2048]{1,0:T(8,128)} %bitcast.61, s32[2,256]{1,0:T(2,128)} %bitcast.62, bf16[1,2048,3200]{2,1,0:T(8,128)(2,1)} %w1.1, ...), custom_call_target="tpu_custom_call" | custom-call | tf_op jit(solution)/shard_map/moe_ring/pallas_call | solution.py:381
  226.4 1.2 slice.15
  228.3 0.3 conditional.1
  228.6 2.3 copy.28
